TPU v7x, 32 devices: a whole 2x2x4 slice. The times are simulated.
32 devices in a mesh: dp: 8 (over y, x, core), seq: 4 (over z).
Axes of the slice: x: 2, y: 2, z: 4, core: 2. Of those that a mesh axis runs over, the one named last changes fastest.
Arguments:
- tokens: bfloat16 [8, 512, 2048], P('dp', 'seq'), may hold values from -6 to 6
- qkv_weight: bfloat16 [3, 2048, 1024], P(None, 'dp', 'seq'), may hold values from -0.125 to 0.125
- qk_scale: float32 [1024], replicated, may hold values from 0.5 to 10
- out_weight: bfloat16 [1024, 2048], P('seq', 'dp'), may hold values from -0.1875 to 0.1875
- mix_rates: float32 [2, 2048], replicated, may hold values from 0.1 to 0.6
- gate_up_weight: bfloat16 [2, 2048, 8192], P(None, 'dp', 'seq'), may hold values from -0.125 to 0.125
- mlp_scales: float32 [2, 8192], P(None, 'seq'), may hold values from 0.5 to 2
- down_weight: bfloat16 [8192, 2048], P('seq', 'dp'), may hold values from -0.0625 to 0.0625
Outputs:
- result: bfloat16 [8, 512, 2048], P('dp', 'seq')
All inputs are finite; a program needn't handle non-finite values.
Results may differ from a plain program's by a relative error of at most 0.015.
The roundings to bfloat16 on the way count: a program that leaves them out, or rounds other values in their place, can miss the bound.
Values may be sent and summed in bfloat16 or wider, within the bound.
No kernel may reach another device: no remote copies, remote signals or barrier semaphores. Data moves between devices by JAX's collectives and lax.ppermute only.
A program may use at most 128 MiB of HBM per device.

v0:
```python
import jax
import jax.numpy as jnp
from jax import lax
from jax.sharding import PartitionSpec as P

HD = 128


def unit_rms(values_in):
    return values_in * lax.rsqrt(jnp.mean(values_in * values_in, axis=-1, keepdims=True) + 1e-06)


def prepare(projected, scale_heads):
    queries = unit_rms(projected[:, 0]) * scale_heads
    key_rows = unit_rms(projected[:, 1]) * scale_heads
    return jnp.stack([queries, key_rows, projected[:, 2]], axis=1).astype(jnp.bfloat16)


def attend(stacked):
    length = stacked.shape[0]
    head_count = stacked.shape[2]
    head_dim = stacked.shape[3]
    block_rows = min(length, 512)
    block_count = length // block_rows
    key_rows = stacked[:, 1]
    value_rows = stacked[:, 2]
    queries = stacked[:, 0].reshape(block_count, block_rows, head_count, head_dim)
    positions = jnp.arange(length, dtype=jnp.int32)
    factor = head_dim ** (-0.5)

    def one_block(inputs):
        block_index, query_block = inputs
        scores = (
            jnp.einsum("qhd,khd->hqk", query_block, key_rows, preferred_element_type=jnp.float32)
            * factor
        )
        query_pos = block_index * block_rows + jnp.arange(block_rows, dtype=jnp.int32)
        allowed = positions[None, :] <= query_pos[:, None]
        scores = jnp.where(allowed[None], scores, -1e30)
        highest = jnp.max(scores, axis=-1, keepdims=True)
        powers = jnp.exp(scores - highest)
        shares = (powers / jnp.sum(powers, axis=-1, keepdims=True)).astype(jnp.bfloat16)
        mixed = jnp.einsum("hqk,khd->qhd", shares, value_rows, preferred_element_type=jnp.float32)
        return mixed.astype(jnp.bfloat16)

    mixed_all = lax.map(one_block, (jnp.arange(block_count, dtype=jnp.int32), queries))
    return mixed_all.reshape(length, head_count, head_dim)


def on_device(
    tokens, qkv_weight, qk_scale, out_weight, mix_rates, gate_up_weight, mlp_scales, down_weight
):
    own_rows = tokens[0]
    head_dim = HD
    normed = unit_rms(own_rows.astype(jnp.float32)).astype(jnp.bfloat16)
    scale_all = qk_scale.reshape(-1, head_dim)
    sequence = lax.all_gather(normed, "seq", axis=0, tiled=True)
    length = sequence.shape[0]
    columns = sequence
    projected = jnp.einsum(
        "td,cdn->tcn",
        columns,
        lax.all_gather(qkv_weight, "dp", axis=1, tiled=True),
        preferred_element_type=jnp.float32,
    )
    local_heads = qkv_weight.shape[2] // head_dim
    scale_local = lax.dynamic_slice_in_dim(
        scale_all, lax.axis_index("seq") * local_heads, local_heads, 0
    )
    stacked = prepare(projected.reshape(length, 3, local_heads, head_dim), scale_local)
    attended = attend(stacked).reshape(length, -1)
    out_cols_all = lax.all_gather(out_weight, "dp", axis=1, tiled=True)
    part_rows = attended
    attention = lax.psum_scatter(
        jnp.dot(part_rows, out_cols_all, preferred_element_type=jnp.float32).astype(jnp.bfloat16),
        "seq",
        scatter_dimension=0,
        tiled=True,
    ).astype(jnp.float32)
    normed_f = normed.astype(jnp.float32)
    middle = unit_rms(normed_f + mix_rates[0] * (unit_rms(attention) - normed_f)).astype(
        jnp.bfloat16
    )
    sequence_mid = lax.all_gather(middle, "seq", axis=0, tiled=True)
    columns = sequence_mid
    gate_up = jnp.einsum(
        "td,cdf->tcf",
        columns,
        lax.all_gather(gate_up_weight, "dp", axis=1, tiled=True),
        preferred_element_type=jnp.float32,
    )
    hidden = (jax.nn.silu(gate_up[:, 0] * mlp_scales[0]) * (gate_up[:, 1] * mlp_scales[1])).astype(
        jnp.bfloat16
    )
    down_all = lax.all_gather(down_weight, "dp", axis=1, tiled=True)
    part_rows = hidden
    feed_out = lax.psum_scatter(
        jnp.dot(part_rows, down_all, preferred_element_type=jnp.float32).astype(jnp.bfloat16),
        "seq",
        scatter_dimension=0,
        tiled=True,
    ).astype(jnp.float32)
    middle_f = middle.astype(jnp.float32)
    result = unit_rms(middle_f + mix_rates[1] * (unit_rms(feed_out) - middle_f)).astype(
        jnp.bfloat16
    )
    return result[None]


def solution(mesh):
    return jax.shard_map(
        on_device,
        mesh=mesh,
        in_specs=(
            P("dp", "seq", None),
            P(None, "dp", "seq"),
            P(),
            P("seq", "dp"),
            P(),
            P(None, "dp", "seq"),
            P(None, "seq"),
            P("seq", "dp"),
        ),
        out_specs=P("dp", "seq", None),
        check_vma=False,
    )
```

profile of v0, /device:TPU:0, one launch (start us, length us, event | category | flops | bytes accessed | tf_op | source)
XLA Modules:
  0.0 430.2 jit_solution(14153458220697589885)
XLA Ops:
  6.5 1.3 fusion.17
  7.8 2.0 fusion.18
  9.9 0.9 copy.9
  11.8 46.6 %all-gather.7.cloned.1.call-done = bf16[512,2048]{1,0:T(8,128)(2,1)} async-done(((bf16[128,2048]{1,0:T(8,128)(2,1)}), bf16[512,2048]{1,0:T(8,128)(2,1)}) %all-gather.7.cloned.1.call-update) | async-done | bytes 2097168 | tf_op jit(solution)/shard_map/all_gather | solution.py:57
  58.4 33.4 %all-gather.9.cloned.1.call-done = bf16[3,2048,256]{1,2,0:T(8,128)(2,1)} async-done(((bf16[3,256,256]{1,2,0:T(8,128)(2,1)}), bf16[3,2048,256]{1,2,0:T(8,128)(2,1)}) %all-gather.9.cloned.1.call-update) | async-done | bytes 3145744 | tf_op jit(solution)/shard_map/all_gather | solution.py:63
  91.8 4.3 %fusion.7 = f32[512,3,256]{0,2,1:T(8,128)S(1)} fusion(bf16[3,2048,256]{1,2,0:T(8,128)(2,1)} %all-gather.9.cloned.1.call-done, bf16[512,2048]{1,0:T(8,128)(2,1)} %all-gather.7.cloned.1.call-done), kind=kOutput, calls=%fused_computation.11 | convolution fusion | flops 1610612736 | bytes 6815744 | tf_op jit(solution)/shard_map/td,cdn->tcn/dot_general | solution.py:60
  96.3 1.1 fusion.63
  97.4 1.3 convolution_convert_fusion.2
  98.7 18.5 %all-gather.11.cloned.1.call-done = bf16[256,2048]{1,0:T(8,128)(2,1)} async-done(((bf16[256,256]{1,0:T(8,128)(2,1)}), bf16[256,2048]{1,0:T(8,128)(2,1)}) %all-gather.11.cloned.1.call-update) | async-done | bytes 1048592 | tf_op jit(solution)/shard_map/all_gather | solution.py:72
  117.2 3.3 convolution_convert_fusion
  121.3 43.1 %reduce-scatter.3.cloned.1.call-done = bf16[128,2048]{1,0:T(8,128)(2,1)} async-done(((bf16[512,2048]{1,0:T(8,128)(2,1)}), bf16[128,2048]{1,0:T(8,128)(2,1)}) %reduce-scatter.3.cloned.1.call-update) | async-done | bytes 524304 | tf_op jit(solution)/shard_map/reduce_scatter | solution.py:74
  164.4 1.2 fusion.14
  165.6 1.5 multiply_reduce_fusion.1
  167.1 2.2 multiply_convert_fusion.1
  170.0 0.7 all-gather.17.cloned.1.call-update
  171.0 43.4 %all-gather.13.cloned.1.call-done = bf16[512,2048]{1,0:T(8,128)(2,1)} async-done(((bf16[128,2048]{1,0:T(8,128)(2,1)}), bf16[512,2048]{1,0:T(8,128)(2,1)}) %all-gather.13.cloned.1.call-update) | async-done | bytes 2097168 | tf_op jit(solution)/shard_map/all_gather | solution.py:84
  214.4 90.3 %all-gather.15.cloned.1.call-done = bf16[2,2048,2048]{2,1,0:T(8,128)(2,1)} async-done(((bf16[2,256,2048]{2,1,0:T(8,128)(2,1)}), bf16[2,2048,2048]{2,1,0:T(8,128)(2,1)}) %all-gather.15.cloned.1.call-update) | async-done | bytes 16777232 | tf_op jit(solution)/shard_map/all_gather | solution.py:89
  304.7 14.9 %fusion.5 = f32[512,2,2048]{2,0,1:T(8,128)} fusion(bf16[2,2048,2048]{2,1,0:T(8,128)(2,1)} %all-gather.15.cloned.1.call-done, bf16[512,2048]{1,0:T(8,128)(2,1)} %all-gather.13.cloned.1.call-done), kind=kOutput, calls=%fused_computation.9 | convolution fusion | flops 8589934592 | bytes 27262976 | tf_op jit(solution)/shard_map/td,cdf->tcf/dot_general | solution.py:86
  319.6 42.9 %all-gather.17.cloned.1.call-done = bf16[2048,2048]{1,0:T(8,128)(2,1)} async-done(((bf16[2048,256]{1,0:T(8,128)(2,1)}), bf16[2048,2048]{1,0:T(8,128)(2,1)}) %all-gather.17.cloned.1.call-update) | async-done | bytes 8388624 | tf_op jit(solution)/shard_map/all_gather | solution.py:95
  362.5 11.9 %convolution_convert_fusion.1 = bf16[512,2048]{1,0:T(8,128)(2,1)} fusion(bf16[2048,2048]{1,0:T(8,128)(2,1)} %all-gather.17.cloned.1.call-done, f32[512,2,2048]{2,0,1:T(8,128)} %fusion.5, f32[2048]{0:T(1024)S(1)} %bitcast.89, f32[2048]{0:T(1024)S(1)} %bitcast.88), kind=kOutput, calls=%fused_computation.8 | convolution fusion | flops 4304404480 | bytes 18890752 | tf_op jit(solution)/shard_map/dot_general | solution.py:98
  374.4 43.8 %reduce-scatter.5.cloned.1.call-done = bf16[128,2048]{1,0:T(8,128)(2,1)} async-done(((bf16[512,2048]{1,0:T(8,128)(2,1)}), bf16[128,2048]{1,0:T(8,128)(2,1)}) %reduce-scatter.5.cloned.1.call-update) | async-done | bytes 524304 | tf_op jit(solution)/shard_map/reduce_scatter | solution.py:97
  418.2 1.2 fusion.16
  419.5 1.5 multiply_reduce_fusion
  421.0 2.3 fusion.22
  (38 shorter events, 2.7 us)
Async XLA Ops:
  6.5 5.1 %copy-start = (f32[1024]{0:T(1024)S(1)}, f32[1024]{0:T(1024)}, u32[]{:S(2)}) copy-start(f32[1024]{0:T(1024)} %param.10) | copy-start | bytes 12292
  6.5 3.4 copy-start.3
  6.5 51.8 %all-gather.7.cloned.1.call-start = ((), (), s32[]{:S(2)}) async-start(), calls=%async_computation.2 | async-start | bytes 2621440 | tf_op jit(solution)/shard_map/all_gather | solution.py:57
  9.8 82.0 %all-gather.9.cloned.1.call-start = ((), (), s32[]{:S(2)}) async-start(), calls=%async_computation.3 | async-start | bytes 3538944 | tf_op jit(solution)/shard_map/all_gather | solution.py:63
  10.9 106.3 %all-gather.11.cloned.1.call-start = ((), (), s32[]{:S(2)}) async-start(), calls=%async_computation.4 | async-start | bytes 1179648 | tf_op jit(solution)/shard_map/all_gather | solution.py:72
  11.6 152.7 %reduce-scatter.3.cloned.1.call-start = ((), (), s32[]{:S(2)}) async-start(), calls=%async_computation.5 | async-start | bytes 2621440 | tf_op jit(solution)/shard_map/reduce_scatter | solution.py:74
  120.5 0.7 copy-start.4
  120.5 45.1 %copy-start.1 = (bf16[1,128,2048]{2,1,0:T(8,128)(2,1)S(1)}, bf16[1,128,2048]{2,1,0:T(8,128)(2,1)}, u32[]{:S(2)}) copy-start(bf16[1,128,2048]{2,1,0:T(8,128)(2,1)} %param.8) | copy-start | bytes 1572868
  120.6 93.8 %all-gather.13.cloned.1.call-start = ((), (), s32[]{:S(2)}) async-start(), calls=%async_computation.6 | async-start | bytes 2621440 | tf_op jit(solution)/shard_map/all_gather | solution.py:84
  169.3 1.6 copy-start.5
  169.4 135.3 %all-gather.15.cloned.1.call-start = ((), (), s32[]{:S(2)}) async-start(), calls=%async_computation.7 | async-start | bytes 18874368 | tf_op jit(solution)/shard_map/all_gather | solution.py:89
  169.9 192.5 %all-gather.17.cloned.1.call-start = ((), (), s32[]{:S(2)}) async-start(), calls=%async_computation.8 | async-start | bytes 9437184 | tf_op jit(solution)/shard_map/all_gather | solution.py:95
  170.7 247.5 %reduce-scatter.5.cloned.1.call-start = ((), (), s32[]{:S(2)}) async-start(), calls=%async_computation.9 | async-start | bytes 2621440 | tf_op jit(solution)/shard_map/reduce_scatter | solution.py:97
  374.4 45.1 %copy-start.2 = (bf16[128,2048]{1,0:T(8,128)(2,1)S(1)}, bf16[128,2048]{1,0:T(8,128)(2,1)}, u32[]{:S(2)}) copy-start(bf16[128,2048]{1,0:T(8,128)(2,1)} %multiply_convert_fusion.1) | copy-start | bytes 1572868
Sparse Core Ops, SparseCore 0:
  10.0 48.3 all-gather.6
  60.3 31.5 all-gather.8
  93.7 23.4 all-gather.10
  120.7 43.6 reduce-scatter.2
  169.5 44.8 all-gather.12
  216.1 88.5 all-gather.14
  306.6 55.8 all-gather.16
  374.5 43.6 reduce-scatter.4
where the time goes:
time: 431 us; the launch traced here: 430 us
  waiting for transfers between devices  364 us (84%)
  matrix products  36.9 us (9%)
  between operations  13.6 us (3%)
  other arithmetic  13.5 us (3%)
    all_gather x1, waiting for transfers between devices, on_device(): lax.all_gather(gate_up_weight, 'dp', axis=1, tiled=True)  90.3 us
    all_gather x1, waiting for transfers between devices, on_device(): sequence = lax.all_gather(normed, 'seq', axis=0, tiled=True)  46.6 us
    reduce_scatter x1, waiting for transfers between devices, on_device(): lax.psum_scatter(jnp.dot(part_rows, down_all, preferred_element_type=jnp....  43.8 us
    all_gather x1, waiting for transfers between devices, on_device(): sequence_mid = lax.all_gather(middle, 'seq', axis=0, tiled=True)  43.4 us
    reduce_scatter x1, waiting for transfers between devices, on_device(): lax.psum_scatter(jnp.dot(part_rows, out_cols_all, preferred_element_type=...  43.1 us
    all_gather x1, waiting for transfers between devices, on_device(): down_all = lax.all_gather(down_weight, 'dp', axis=1, tiled=True)  42.9 us
    all_gather x1, waiting for transfers between devices, on_device(): lax.all_gather(qkv_weight, 'dp', axis=1, tiled=True)  33.4 us
    all_gather x1, waiting for transfers between devices, on_device(): out_cols_all = lax.all_gather(out_weight, 'dp', axis=1, tiled=True)  18.5 us
  transfers between devices with their start and end apart: 8, of which 8 were waited for; matrix products, arithmetic and copies ran while one was open for 5% of the time, Pallas kernels for 0%

commit v1 on v0

--- a/solution.py
+++ b/solution.py
@@ -2,6 +2,7 @@
 import jax.numpy as jnp
 from jax import lax
 from jax.sharding import PartitionSpec as P
+from jax.lax import axis_index, axis_size, ppermute
 
 HD = 128
 
@@ -50,6 +51,22 @@
 def on_device(
     tokens, qkv_weight, qk_scale, out_weight, mix_rates, gate_up_weight, mlp_scales, down_weight
 ):
+
+    def place_edges_on(vector, work_x):
+        opened, left_arr, piece_now = (axis_size("dp"), axis_index("dp"), vector.shape[1])
+        inbox = tuple(((idx, (idx + 1) % opened) for idx in range(opened)))
+        seen = tuple(((idx, (idx - 1) % opened) for idx in range(opened)))
+        n_now = opened // 2
+        p_next = v_now = vector
+        then = work_x(vector, left_arr * piece_now)
+        for rr in range(1, n_now + 1):
+            p_next = ppermute(p_next, axis_name="dp", perm=inbox)
+            if rr < opened - n_now:
+                v_now = ppermute(v_now, axis_name="dp", perm=seen)
+                then = then + work_x(v_now, (left_arr + rr) % opened * piece_now)
+            then = then + work_x(p_next, (left_arr - rr) % opened * piece_now)
+        return then
+
     own_rows = tokens[0]
     head_dim = HD
     normed = unit_rms(own_rows.astype(jnp.float32)).astype(jnp.bfloat16)
@@ -83,11 +100,14 @@
     )
     sequence_mid = lax.all_gather(middle, "seq", axis=0, tiled=True)
     columns = sequence_mid
-    gate_up = jnp.einsum(
-        "td,cdf->tcf",
-        columns,
-        lax.all_gather(gate_up_weight, "dp", axis=1, tiled=True),
-        preferred_element_type=jnp.float32,
+    gate_up = place_edges_on(
+        gate_up_weight,
+        lambda part, start: jnp.einsum(
+            "td,cdf->tcf",
+            lax.dynamic_slice_in_dim(columns, start, part.shape[1], axis=1),
+            part,
+            preferred_element_type=jnp.float32,
+        ),
     )
     hidden = (jax.nn.silu(gate_up[:, 0] * mlp_scales[0]) * (gate_up[:, 1] * mlp_scales[1])).astype(
         jnp.bfloat16

time: 431 us -> 480 us (1.11)
  matrix products: 36.9 us -> 85.4 us
  waiting for transfers between devices: 364 us -> 356 us
  starting transfers between devices: 0.46 us -> 7.18 us
    ppermute x0 -> x7, waiting for transfers between devices: none -> 163 us  [the longest x4 160 us: place_edges_on(): p_next = ppermute(p_next, axis_name='dp', perm=inbox)]
    all_gather x1 -> x0, waiting for transfers between devices: 90.3 us -> none  [on_device(): lax.all_gather(gate_up_weight, 'dp', axis=1, tiled=True)]
    dot_general x1 -> x8, matrix products: 14.9 us -> 63.3 us  [on_device(): jnp.einsum('td,cdf->tcf', lax.dynamic_slice_in_dim(columns, start, part.s...]
    all_gather x1, waiting for transfers between devices: 43.4 us -> 0.01 us  [on_device(): sequence_mid = lax.all_gather(middle, 'seq', axis=0, tiled=True)]
    all_gather x1, waiting for transfers between devices: 42.9 us -> 0.01 us  [on_device(): down_all = lax.all_gather(down_weight, 'dp', axis=1, tiled=True)]
    ppermute x0 -> x7, starting transfers between devices: none -> 6.93 us  [the longest x3 6.87 us: place_edges_on(): v_now = ppermute(v_now, axis_name='dp', perm=seen)]
    reduce_scatter x1, waiting for transfers between devices: 43.8 us -> 50.1 us  [on_device(): lax.psum_scatter(jnp.dot(part_rows, down_all, preferred_element_type=jnp....]
  transfers between devices with their start and end apart: 8 -> 14, of which waited for: 8 -> 9; matrix products, arithmetic and copies ran while one was open for 5% -> 15% of each run, Pallas kernels for 0% -> 0%
where the time goes in v1:
time: 480 us; the launch traced here: 479 us
  waiting for transfers between devices  356 us (74%)
  matrix products  85.4 us (18%)
  other arithmetic  13.7 us (3%)
  between operations  13.6 us (3%)
  starting transfers between devices  7.18 us (1%)
    ppermute x4, waiting for transfers between devices, place_edges_on(): p_next = ppermute(p_next, axis_name='dp', perm=inbox)  160 us
    dot_general x8, matrix products, on_device(): jnp.einsum('td,cdf->tcf', lax.dynamic_slice_in_dim(columns, start, part.s...  63.3 us
    reduce_scatter x1, waiting for transfers between devices, on_device(): lax.psum_scatter(jnp.dot(part_rows, down_all, preferred_element_type=jnp....  50.1 us
    all_gather x1, waiting for transfers between devices, on_device(): sequence = lax.all_gather(normed, 'seq', axis=0, tiled=True)  46.6 us
    reduce_scatter x1, waiting for transfers between devices, on_device(): lax.psum_scatter(jnp.dot(part_rows, out_cols_all, preferred_element_type=...  43.1 us
    all_gather x1, waiting for transfers between devices, on_device(): lax.all_gather(qkv_weight, 'dp', axis=1, tiled=True)  33.4 us
    all_gather x1, waiting for transfers between devices, on_device(): out_cols_all = lax.all_gather(out_weight, 'dp', axis=1, tiled=True)  18.5 us
    dot_general x1, matrix products, on_device(): jnp.dot(part_rows, down_all, preferred_element_type=jnp.float32)  12 us
  transfers between devices with their start and end apart: 14, of which 9 were waited for; matrix products, arithmetic and copies ran while one was open for 15% of the time, Pallas kernels for 0%

profile of v1, /device:TPU:0, one launch (start us, length us, event | category | flops | bytes accessed | tf_op | source)
XLA Modules:
  0.0 479.0 jit_solution(10140182769900644422)
XLA Ops:
  11.8 46.6 %all-gather.6.cloned.1.call-done = bf16[512,2048]{1,0:T(8,128)(2,1)} async-done(((bf16[128,2048]{1,0:T(8,128)(2,1)}), bf16[512,2048]{1,0:T(8,128)(2,1)}) %all-gather.6.cloned.1.call-update) | async-done | bytes 2097168 | tf_op jit(solution)/shard_map/all_gather | solution.py:74
  58.4 33.4 %all-gather.8.cloned.1.call-done = bf16[3,2048,256]{1,2,0:T(8,128)(2,1)} async-done(((bf16[3,256,256]{1,2,0:T(8,128)(2,1)}), bf16[3,2048,256]{1,2,0:T(8,128)(2,1)}) %all-gather.8.cloned.1.call-update) | async-done | bytes 3145744 | tf_op jit(solution)/shard_map/all_gather | solution.py:80
  91.8 4.3 fusion.5
  98.7 18.5 %all-gather.10.cloned.1.call-done = bf16[256,2048]{1,0:T(8,128)(2,1)} async-done(((bf16[256,256]{1,0:T(8,128)(2,1)}), bf16[256,2048]{1,0:T(8,128)(2,1)}) %all-gather.10.cloned.1.call-update) | async-done | bytes 1048592 | tf_op jit(solution)/shard_map/all_gather | solution.py:89
  117.2 3.3 convolution_convert_fusion
  121.3 43.1 %reduce-scatter.3.cloned.1.call-done = bf16[128,2048]{1,0:T(8,128)(2,1)} async-done(((bf16[512,2048]{1,0:T(8,128)(2,1)}), bf16[128,2048]{1,0:T(8,128)(2,1)}) %reduce-scatter.3.cloned.1.call-update) | async-done | bytes 524304 | tf_op jit(solution)/shard_map/reduce_scatter | solution.py:91
  167.3 2.2 multiply_convert_fusion.1
  170.3 2.6 collective-permute-start
  172.9 44.4 %collective-permute-done.1 = bf16[2,256,2048]{2,1,0:T(8,128)(2,1)S(1)} collective-permute-done((bf16[2,256,2048]{2,1,0:T(8,128)(2,1)S(1)}, bf16[2,256,2048]{2,1,0:T(8,128)(2,1)S(1)}, u32[]{:S(2)}, u32[]{:S(2)}) %collective-permute-start.1) | collective-permute-done | bytes 2097184 | tf_op jit(solution)/shard_map/ppermute | solution.py:63
  220.1 75.3 %collective-permute-done.3 = bf16[2,256,2048]{2,1,0:T(8,128)(2,1)} collective-permute-done((bf16[2,256,2048]{2,1,0:T(8,128)(2,1)S(1)}, bf16[2,256,2048]{2,1,0:T(8,128)(2,1)}, u32[]{:S(2)}, u32[]{:S(2)}) %collective-permute-start.3) | collective-permute-done | bytes 2097184 | tf_op jit(solution)/shard_map/ppermute | solution.py:63
  295.4 3.6 collective-permute-done.2
  299.0 2.8 collective-permute-start.4
  301.8 39.8 %collective-permute-done.5 = bf16[2,256,2048]{2,1,0:T(8,128)(2,1)} collective-permute-done((bf16[2,256,2048]{2,1,0:T(8,128)(2,1)}, bf16[2,256,2048]{2,1,0:T(8,128)(2,1)}, u32[]{:S(2)}, u32[]{:S(2)}) %collective-permute-start.5) | collective-permute-done | bytes 2097184 | tf_op jit(solution)/shard_map/ppermute | solution.py:63
  341.7 6.3 %fusion.33 = f32[512,2,2048]{2,0,1:T(8,128)} fusion(bf16[2,256,2048]{2,1,0:T(8,128)(2,1)} %collective-permute-done.3, bf16[512,2048]{1,0:T(8,128)(2,1)} %all-gather.12.cloned.1.call-done, s32[]{:T(128)S(6)} %select_n.73), kind=kOutput, calls=%fused_computation.58 | convolution fusion | flops 1073741824 | bytes 10747908 | tf_op jit(solution)/shard_map/td,cdf->tcf/dot_general | solution.py:105
  348.0 6.2 %fusion.35 = f32[512,2,2048]{2,0,1:T(8,128)} fusion(bf16[2,256,2048]{2,1,0:T(8,128)(2,1)} %collective-permute-done.2, bf16[512,2048]{1,0:T(8,128)(2,1)S(1)} %copy-done.7, s32[]{:T(128)S(6)} %select_n.71), kind=kOutput, calls=%fused_computation.60 | convolution fusion | flops 1073741824 | bytes 10747908 | tf_op jit(solution)/shard_map/td,cdf->tcf/dot_general | solution.py:105
  354.2 4.5 fusion.37
  358.7 6.1 %fusion.39 = f32[512,2,2048]{2,0,1:T(8,128)} fusion(bf16[2,256,2048]{2,1,0:T(8,128)(2,1)} %collective-permute-done, bf16[512,2048]{1,0:T(8,128)(2,1)S(1)} %copy-done.7, s32[]{:T(128)S(6)} %select_n.67), kind=kOutput, calls=%fused_computation.64 | convolution fusion | flops 1073741824 | bytes 10747908 | tf_op jit(solution)/shard_map/td,cdf->tcf/dot_general | solution.py:105
  364.8 6.1 %fusion.29 = f32[512,2,2048]{2,0,1:T(8,128)} fusion(bf16[2,256,2048]{2,1,0:T(8,128)(2,1)} %collective-permute-done.5, bf16[512,2048]{1,0:T(8,128)(2,1)S(1)} %copy-done.7, s32[]{:T(128)S(6)} %select_n.77), kind=kOutput, calls=%fused_computation.54 | convolution fusion | flops 1073741824 | bytes 10747908 | tf_op jit(solution)/shard_map/td,cdf->tcf/dot_general | solution.py:105
  370.9 4.5 fusion.41
  375.3 6.1 %fusion.31 = f32[512,2,2048]{2,0,1:T(8,128)} fusion(bf16[2,256,2048]{2,1,0:T(8,128)(2,1)} %collective-permute-done.4, bf16[512,2048]{1,0:T(8,128)(2,1)S(1)} %copy-done.7, s32[]{:T(128)S(6)} %select_n.75), kind=kOutput, calls=%fused_computation.56 | convolution fusion | flops 1073741824 | bytes 10747908 | tf_op jit(solution)/shard_map/td,cdf->tcf/dot_general | solution.py:105
  381.4 23.6 %add_add_fusion = f32[512,2,2048]{2,0,1:T(8,128)} fusion(f32[512,2,2048]{2,0,1:T(8,128)} %fusion.29, f32[512,2,2048]{2,0,1:T(8,128)} %fusion.31, f32[512,2,2048]{2,0,1:T(8,128)} %fusion.33, f32[512,2,2048]{2,0,1:T(8,128)} %fusion.35, f32[512,2,2048]{2,0,1:T(8,128)} %fusion.37, f32[512,2,2048]{2,0,1:T(8,128)} %fusion.41, f32[512,2,2048]{2,0,1:T(8,128)} %fusion.39, ...), kind=kOutput, calls=%fused_computation.1 | convolution fusion | flops 1088421888 | bytes 69468160 | tf_op jit(solution)/shard_map/td,cdf->tcf/dot_general | solution.py:105
  405.0 12.0 %convolution_convert_fusion.1 = bf16[512,2048]{1,0:T(8,128)(2,1)} fusion(bf16[2048,2048]{1,0:T(8,128)(2,1)} %all-gather.14.cloned.1.call-done, f32[512,2,2048]{2,0,1:T(8,128)} %add_add_fusion, f32[2048]{0:T(1024)S(1)} %bitcast.117, f32[2048]{0:T(1024)S(1)} %bitcast.116), kind=kOutput, calls=%fused_computation.9 | convolution fusion | flops 4304404480 | bytes 18890752 | tf_op jit(solution)/shard_map/dot_general | solution.py:118
  417.0 50.1 %reduce-scatter.5.cloned.1.call-done = bf16[128,2048]{1,0:T(8,128)(2,1)} async-done(((bf16[512,2048]{1,0:T(8,128)(2,1)}), bf16[128,2048]{1,0:T(8,128)(2,1)}) %reduce-scatter.5.cloned.1.call-update) | async-done | bytes 524304 | tf_op jit(solution)/shard_map/reduce_scatter | solution.py:117
  469.8 2.3 fusion.20
  (66 shorter events, 17.6 us)
Async XLA Ops:
  6.5 5.1 %copy-start = (f32[1024]{0:T(1024)S(1)}, f32[1024]{0:T(1024)}, u32[]{:S(2)}) copy-start(f32[1024]{0:T(1024)} %param.10) | copy-start | bytes 12292
  6.5 3.4 copy-start.8
  6.5 51.8 %all-gather.6.cloned.1.call-start = ((), (), s32[]{:S(2)}) async-start(), calls=%async_computation.2 | async-start | bytes 2621440 | tf_op jit(solution)/shard_map/all_gather | solution.py:74
  9.8 82.0 %all-gather.8.cloned.1.call-start = ((), (), s32[]{:S(2)}) async-start(), calls=%async_computation.3 | async-start | bytes 3538944 | tf_op jit(solution)/shard_map/all_gather | solution.py:80
  10.9 106.4 %all-gather.10.cloned.1.call-start = ((), (), s32[]{:S(2)}) async-start(), calls=%async_computation.4 | async-start | bytes 1179648 | tf_op jit(solution)/shard_map/all_gather | solution.py:89
  11.6 152.8 %reduce-scatter.3.cloned.1.call-start = ((), (), s32[]{:S(2)}) async-start(), calls=%async_computation.5 | async-start | bytes 2621440 | tf_op jit(solution)/shard_map/reduce_scatter | solution.py:91
  120.5 45.1 %copy-start.2 = (bf16[1,128,2048]{2,1,0:T(8,128)(2,1)S(1)}, bf16[1,128,2048]{2,1,0:T(8,128)(2,1)}, u32[]{:S(2)}) copy-start(bf16[1,128,2048]{2,1,0:T(8,128)(2,1)} %param.8) | copy-start | bytes 1572868
  120.6 221.1 %all-gather.12.cloned.1.call-start = ((), (), s32[]{:S(2)}) async-start(), calls=%async_computation.6 | async-start | bytes 2621440 | tf_op jit(solution)/shard_map/all_gather | solution.py:101
  165.6 4.6 copy-start.4
  165.6 129.8 %copy-start.10 = (f32[2,2048]{1,0:T(2,128)S(1)}, f32[2,2048]{1,0:T(2,128)}, u32[]{:S(2)}) copy-start(f32[2,2048]{1,0:T(2,128)} %param.14) | copy-start | bytes 49156
  169.6 235.5 %all-gather.14.cloned.1.call-start = ((), (), s32[]{:S(2)}) async-start(), calls=%async_computation.7 | async-start | bytes 9437184 | tf_op jit(solution)/shard_map/all_gather | solution.py:115
  170.1 297.0 %reduce-scatter.5.cloned.1.call-start = ((), (), s32[]{:S(2)}) async-start(), calls=%async_computation.8 | async-start | bytes 2621440 | tf_op jit(solution)/shard_map/reduce_scatter | solution.py:117
  170.2 47.1 %collective-permute-start.1 = (bf16[2,256,2048]{2,1,0:T(8,128)(2,1)S(1)}, bf16[2,256,2048]{2,1,0:T(8,128)(2,1)S(1)}, u32[]{:S(2)}, u32[]{:S(2)}) collective-permute-start(bf16[2,256,2048]{2,1,0:T(8,128)(2,1)S(1)} %copy-done.4), channel_id=1, source_target_pairs={{0,4},{4,8},{8,12},{12,16},{16,20},{20,24},{24,28},{28,0},{1,5},{5... | collective-permute-start | bytes 6291464 | tf_op jit(solution)/shard_map/ppermute | solution.py:63
  170.3 47.0 %collective-permute-start = (bf16[2,256,2048]{2,1,0:T(8,128)(2,1)S(1)}, bf16[2,256,2048]{2,1,0:T(8,128)(2,1)}, u32[]{:S(2)}, u32[]{:S(2)}) collective-permute-start(bf16[2,256,2048]{2,1,0:T(8,128)(2,1)S(1)} %copy-done.4), channel_id=1, source_target_pairs={{0,28},{4,0},{8,4},{12,8},{16,12},{20,16},{24,20},{28,24},{1,29},{... | collective-permute-start | bytes 6291464 | tf_op jit(solution)/shard_map/ppermute | solution.py:65
  217.3 1.3 copy-start.5
  217.3 78.1 %collective-permute-start.3 = (bf16[2,256,2048]{2,1,0:T(8,128)(2,1)S(1)}, bf16[2,256,2048]{2,1,0:T(8,128)(2,1)}, u32[]{:S(2)}, u32[]{:S(2)}) collective-permute-start(bf16[2,256,2048]{2,1,0:T(8,128)(2,1)S(1)} %collective-permute-done.1), channel_id=1, source_target_pairs={{0,4},{4,8},{8,12},{12,16},{16,20},{20,24},{24,28},{28,0},{1,5},{5... | collective-permute-start | bytes 6291464 | tf_op jit(solution)/shard_map/ppermute | solution.py:63
  218.6 80.4 %collective-permute-start.2 = (bf16[2,256,2048]{2,1,0:T(8,128)(2,1)}, bf16[2,256,2048]{2,1,0:T(8,128)(2,1)}, u32[]{:S(2)}, u32[]{:S(2)}) collective-permute-start(bf16[2,256,2048]{2,1,0:T(8,128)(2,1)} %collective-permute-done), channel_id=1, source_target_pairs={{0,28},{4,0},{8,4},{12,8},{16,12},{20,16},{24,20},{28,24},{1,29},{... | collective-permute-start | bytes 6291464 | tf_op jit(solution)/shard_map/ppermute | solution.py:65
  295.4 46.3 %collective-permute-start.5 = (bf16[2,256,2048]{2,1,0:T(8,128)(2,1)}, bf16[2,256,2048]{2,1,0:T(8,128)(2,1)}, u32[]{:S(2)}, u32[]{:S(2)}) collective-permute-start(bf16[2,256,2048]{2,1,0:T(8,128)(2,1)} %collective-permute-done.3), channel_id=1, source_target_pairs={{0,4},{4,8},{8,12},{12,16},{16,20},{20,24},{24,28},{28,0},{1,5},{5... | collective-permute-start | bytes 6291464 | tf_op jit(solution)/shard_map/ppermute | solution.py:63
  299.0 76.3 %collective-permute-start.4 = (bf16[2,256,2048]{2,1,0:T(8,128)(2,1)}, bf16[2,256,2048]{2,1,0:T(8,128)(2,1)}, u32[]{:S(2)}, u32[]{:S(2)}) collective-permute-start(bf16[2,256,2048]{2,1,0:T(8,128)(2,1)} %collective-permute-done.2), channel_id=1, source_target_pairs={{0,28},{4,0},{8,4},{12,8},{16,12},{20,16},{24,20},{28,24},{1,29},{... | collective-permute-start | bytes 6291464 | tf_op jit(solution)/shard_map/ppermute | solution.py:65
  341.7 39.7 %collective-permute-start.6 = (bf16[2,256,2048]{2,1,0:T(8,128)(2,1)}, bf16[2,256,2048]{2,1,0:T(8,128)(2,1)}, u32[]{:S(2)}, u32[]{:S(2)}) collective-permute-start(bf16[2,256,2048]{2,1,0:T(8,128)(2,1)} %collective-permute-done.5), channel_id=1, source_target_pairs={{0,4},{4,8},{8,12},{12,16},{16,20},{20,24},{24,28},{28,0},{1,5},{5... | collective-permute-start | bytes 6291464 | tf_op jit(solution)/shard_map/ppermute | solution.py:63
  341.7 6.3 %copy-start.7 = (bf16[512,2048]{1,0:T(8,128)(2,1)S(1)}, bf16[512,2048]{1,0:T(8,128)(2,1)}, u32[]{:S(2)}) copy-start(bf16[512,2048]{1,0:T(8,128)(2,1)} %all-gather.12.cloned.1.call-done) | copy-start | bytes 6291460
  348.0 6.2 %copy-start.6 = (bf16[2,256,2048]{2,1,0:T(8,128)(2,1)S(1)}, bf16[2,256,2048]{2,1,0:T(8,128)(2,1)}, u32[]{:S(2)}) copy-start(bf16[2,256,2048]{2,1,0:T(8,128)(2,1)} %copy-done.5) | copy-start | bytes 6291460
  417.0 51.4 %copy-start.3 = (bf16[128,2048]{1,0:T(8,128)(2,1)S(1)}, bf16[128,2048]{1,0:T(8,128)(2,1)}, u32[]{:S(2)}) copy-start(bf16[128,2048]{1,0:T(8,128)(2,1)} %multiply_convert_fusion.1) | copy-start | bytes 1572868
  417.0 55.2 %copy-start.1 = (f32[1024]{0:T(1024)S(1)}, f32[1024]{0:T(1024)}, u32[]{:S(2)}) copy-start(f32[1024]{0:T(1024)} %param.10) | copy-start | bytes 12292
  (1 other events, 0.7 us)
Sparse Core Ops, SparseCore 0:
  10.0 48.3 all-gather.5
  60.3 31.5 all-gather.7
  93.7 23.4 all-gather.9
  120.7 43.6 reduce-scatter.2
  169.7 44.8 all-gather.11
  216.3 86.5 all-gather.13
  417.1 49.9 reduce-scatter.4
